TPU v7x, 32 devices: a whole 2x2x4 slice. The times are simulated.
32 devices in a mesh: section: 4 (over x, core), ctx: 4 (over z), tp: 2 (over y).
Axes of the slice: x: 2, y: 2, z: 4, core: 2. Of those that a mesh axis runs over, the one named last changes fastest.
Arguments:
- head_input: bfloat16 [4, 1536, 8192], P('section', 'ctx', 'tp'), may hold values from -6 to 6
- gate_input: bfloat16 [4, 1536, 8192], P('section', 'ctx', 'tp'), may hold values from -6 to 6
- b_input: bfloat16 [4, 1536, 1024], P('section', 'ctx', 'tp'), may hold values from -0.52734375 to 0.52734375
- c_input: bfloat16 [4, 1536, 1024], P('section', 'ctx', 'tp'), may hold values from -0.52734375 to 0.52734375
- step_raw: float32 [4, 1536, 128], P('section', 'ctx', 'tp'), may hold values from -6 to 5
- step_bias: float32 [4, 128], P('section', 'tp'), may hold values from -1 to 0.5
- decay_rate: float32 [4, 128], P('section', 'tp'), may hold values from 0.00032552083 to 0.12, as said below
- skip_scale: float32 [4, 128], P('section', 'tp'), may hold values from 0.5 to 2
- norm_gain: float32 [4, 8192], P('section', 'tp'), may hold values from 0.1 to 1.9
- out_weight: bfloat16 [4, 8192, 4096], P('section', 'tp'), may hold values from -0.09375 to 0.09375
- residual: bfloat16 [4, 1536, 4096], P('section', 'ctx', 'tp'), may hold values from -6 to 6
Outputs:
- next_input: bfloat16 [4, 1536, 4096], P('section', 'ctx', 'tp')
Inputs may be any that keep to these rules, and one draw needn't show every extreme that they name: `decay_rate`: positive decay rates per head.
All inputs are finite; a program needn't handle non-finite values.
Results may differ from a plain program's by a relative error of at most 0.017.
Values may be sent and summed in bfloat16 or wider, within the bound.
A program may use at most 128 MiB of HBM per device.

v0:
```python
import jax
import jax.numpy as jnp
from jax import lax
from jax.sharding import PartitionSpec as P

HEAD_DIM = 64
STATE = 128
BLOCK = 128


def carried_in(array, axis, join, neutral):
    place = lax.axis_index(axis)
    gathered = jax.tree.map(
        lambda a, kind: lax.all_gather(a.astype(kind), axis), array, (jnp.bfloat16, jnp.bfloat16)
    )
    state = jax.tree.map(lambda a, e: jnp.zeros_like(a) + jnp.asarray(e, a.dtype), array, neutral)

    def one(lap, state):
        return join(
            state,
            jax.tree.map(
                lambda a, own: lax.dynamic_index_in_dim(a, lap, 0, False).astype(own.dtype),
                gathered,
                array,
            ),
        )

    return lax.fori_loop(0, place, one, state)


def passed_along(block, axis, distance):
    devices = range(lax.axis_size(axis))
    route = [((i - distance) % len(devices), i) for i in devices]
    return lax.ppermute(block, axis, route)


def link_states(earlier, latter):
    return (earlier[0] + latter[0], jnp.exp(latter[0])[:, None, None] * earlier[1] + latter[1])


def pass_blocks(start_state, out_map, block_state, block_total):

    def block_step(carried, items):
        map_blk, state_blk, total_blk = items
        output = jnp.einsum(
            "thn,hnp->thp",
            map_blk,
            carried.astype(jnp.bfloat16),
            preferred_element_type=jnp.float32,
        )
        carried = jnp.exp(total_blk)[:, None, None] * carried + state_blk
        return (carried, output)

    return lax.scan(block_step, start_state, (out_map, block_state, block_total))


def on_device(
    head_input,
    gate_input,
    b_input,
    c_input,
    step_raw,
    step_bias,
    decay_rate,
    skip_scale,
    norm_gain,
    out_weight,
    residual,
):
    highest = lax.Precision.HIGHEST
    length = head_input.shape[1]
    heads_local = step_raw.shape[2]
    groups_local = b_input.shape[2] // STATE
    repeats = heads_local // groups_local
    blocks = length // BLOCK
    values_low = head_input[0].reshape(blocks, BLOCK, heads_local, HEAD_DIM)
    b_low = b_input[0].reshape(blocks, BLOCK, groups_local, STATE)
    c_low = c_input[0].reshape(blocks, BLOCK, groups_local, STATE)
    b_heads = jnp.repeat(b_low, repeats, axis=2).astype(jnp.float32)
    c_heads = jnp.repeat(c_low, repeats, axis=2).astype(jnp.float32)
    steps = jax.nn.softplus(step_raw[0] + step_bias[0][None, :])
    logdecay = (-decay_rate[0][None, :] * steps).reshape(blocks, BLOCK, heads_local)
    steps = steps.reshape(blocks, BLOCK, heads_local)
    cumulative = jnp.cumsum(logdecay, axis=1)
    cum_heads = cumulative.transpose(0, 2, 1)
    step_heads = steps.transpose(0, 2, 1)
    lower_mask = jnp.tril(jnp.ones((BLOCK, BLOCK), dtype=jnp.bool_))[None, None]
    log_gap = cum_heads[:, :, :, None] - cum_heads[:, :, None, :]
    decays = jnp.where(lower_mask, jnp.exp(jnp.where(lower_mask, log_gap, 0.0)), 0.0)
    scores = jnp.repeat(
        jnp.einsum("ktgn,ksgn->kgts", c_low, b_low, preferred_element_type=jnp.float32),
        repeats,
        axis=1,
    )
    weights = (scores * decays * step_heads[:, :, None, :]).astype(jnp.bfloat16)
    y_diag = jnp.einsum("khts,kshp->kthp", weights, values_low, preferred_element_type=jnp.float32)
    end_weight = jnp.exp(cum_heads[:, :, -1:] - cum_heads) * step_heads
    in_map = (end_weight.transpose(0, 2, 1)[:, :, :, None] * b_heads).astype(jnp.bfloat16)
    block_state = jnp.einsum(
        "kshn,kshp->khnp", in_map, values_low, preferred_element_type=jnp.float32
    )
    block_total = cum_heads[:, :, -1]
    device_total = jnp.sum(block_total, axis=0)
    out_map = (c_heads * jnp.exp(cumulative)[:, :, :, None]).astype(jnp.bfloat16)
    empty_state = jnp.zeros((heads_local, STATE, HEAD_DIM), jnp.float32)
    suffix = jnp.cumsum(block_total[::-1], axis=0)[::-1] - block_total
    device_state = jnp.einsum("kh,khnp->hnp", jnp.exp(suffix), block_state, precision=highest)
    prefix = carried_in(
        (device_total, device_state),
        "ctx",
        link_states,
        (jnp.zeros_like(device_total), empty_state),
    )
    _, y_off = pass_blocks(prefix[1], out_map, block_state, block_total)
    scan_out = y_diag + y_off + skip_scale[0][None, None, :, None] * values_low.astype(jnp.float32)
    scan_out = scan_out.reshape(length, heads_local * HEAD_DIM)
    gated = scan_out * jax.nn.silu(gate_input[0].astype(jnp.float32))
    grouped = gated.reshape(length, groups_local, -1)
    mean_square = jnp.mean(grouped * grouped, axis=-1, keepdims=True)
    normed = (grouped * lax.rsqrt(mean_square + 1e-05)).reshape(length, heads_local * HEAD_DIM)
    normed = (normed * norm_gain[0][None, :]).astype(jnp.bfloat16)
    weight = out_weight[0]
    partial_value = jnp.dot(normed, weight, preferred_element_type=jnp.float32)
    mixed = lax.psum_scatter(
        partial_value.astype(jnp.bfloat16), "tp", scatter_dimension=1, tiled=True
    ).astype(jnp.float32)
    result = (residual[0].astype(jnp.float32) + mixed).astype(jnp.bfloat16)
    arrived = passed_along(result, "section", 1)
    return arrived[None]


def solution(mesh):
    placed = (
        P("section", "ctx", "tp"),
        P("section", "ctx", "tp"),
        P("section", "ctx", "tp"),
        P("section", "ctx", "tp"),
        P("section", "ctx", "tp"),
        P("section", "tp"),
        P("section", "tp"),
        P("section", "tp"),
        P("section", "tp"),
        P("section", "tp", None),
        P("section", "ctx", "tp"),
    )
    return jax.shard_map(
        on_device, mesh=mesh, in_specs=placed, out_specs=P("section", "ctx", "tp"), check_vma=False
    )
```

profile of v0, /device:TPU:26, one launch (start us, length us, event | category | flops | bytes accessed | tf_op | source)
XLA Modules:
  0.0 310.4 jit_solution(4402739480602516)
XLA Ops:
  12.7 1.7 copy.51
  16.5 7.8 %reshape.153 = bf16[3,128,64,64]{3,2,1,0:T(8,128)(2,1)} reshape(bf16[1,384,4096]{2,1,0:T(8,128)(2,1)S(1)} %copy-done.3) | data formatting | bytes 6291456 | tf_op jit(solution)/shard_map/reshape;squeeze | solution.py:76
  24.3 8.0 %copy.50 = bf16[3,128,64,64]{1,3,2,0:T(8,128)(2,1)S(1)} copy(bf16[3,128,64,64]{3,2,1,0:T(8,128)(2,1)} %reshape.153) | data formatting | bytes 6291456 | tf_op jit(solution)/shard_map/reshape;squeeze | solution.py:76
  32.3 3.4 %broadcast_in_dim.58 = f32[3,128,4,16,128]{4,1,3,2,0:T(8,128)S(1)} broadcast(f32[3,128,4,128]{3,1,2,0:T(8,128)} %copy.52), dimensions={0,1,2,4} | broadcast | bytes 13369344 | tf_op jit(solution)/shard_map/broadcast_in_dim | solution.py:79
  35.8 8.4 %multiply_reduce_fusion = (bf16[64,128,64]{1,2,0:T(8,128)(2,1)}, f32[3,64,128,64]{2,3,1,0:T(8,128)}) fusion(f32[64,3]{0,1:T(4,128)S(1)} %exponential_bitcast_fusion.1, bf16[3,128,64,64]{1,3,2,0:T(8,128)(2,1)S(1)} %copy.50, f32[3,128,64,128]{3,1,2,0:T(8,128)S(1)} %bitcast.77, f32[3,128,64]{1,2,0:T(8,128)S(1)} %copy-done.6), kind=kOutput, calls=%fused_computation.22 | convolution fusion | flops 411566080 | bytes 23167744 | tf_op jit(solution)/shard_map/kshn,kshp->khnp/dot_general | solution.py:99
  47.4 8.1 %all-reduce = bf16[256]{0:T(256)(128)(2,1)S(1)} all-reduce(bf16[256]{0:T(256)(128)(2,1)S(1)} %dynamic-update-slice), channel_id=2, replica_groups=mesh['section'=4,'ctx'=4,'tp'=2] {'ctx'}, use_global_device_ids=true, to_apply=%add | all-reduce | flops 256 | bytes 1024
  58.4 1.7 copy.48
  60.1 5.4 %copy.60 = f32[1,384,4096]{1,2,0:T(8,128)} copy(bf16[1,384,4096]{2,1,0:T(8,128)(2,1)} %param.16) | data formatting | bytes 9437184 | tf_op jit(solution)/shard_map/convert_element_type | solution.py:117
  65.5 10.4 %reshape.143 = f32[3,128,64,64]{1,0,3,2:T(4,128)} reshape(f32[1,384,4096]{1,2,0:T(8,128)} %copy.60) | data formatting | bytes 12582912 | tf_op jit(solution)/shard_map/convert_element_type | solution.py:117
  80.7 5.5 %multiply_convert_fusion = bf16[3,128,64,128]{3,1,2,0:T(8,128)(2,1)} fusion(f32[3,128,64,128]{3,1,2,0:T(8,128)S(1)} %bitcast.78, f32[3,128,64]{1,2,0:T(8,128)S(1)} %copy.56), kind=kLoop, calls=%fused_computation.15 | loop fusion | flops 6291456 | bytes 18972672 | tf_op jit(solution)/shard_map/convert_element_type | solution.py:104
  86.2 37.3 %all-gather.4.cloned.1.call-done = bf16[256,128,64]{1,2,0:T(8,128)(2,1)} async-done(((bf16[64,128,64]{1,2,0:T(8,128)(2,1)}), bf16[256,128,64]{1,2,0:T(8,128)(2,1)}) %all-gather.4.cloned.1.call-update) | async-done | bytes 4194320 | tf_op jit(solution)/shard_map/all_gather | solution.py:14
  123.5 2.5 broadcast_in_dim.57
  126.0 21.0 %while.24 = (s32[]{:T(128)}, f32[64,128,64]{2,1,0:T(8,128)}, s32[]{:T(128)}, bf16[4,64]{1,0:T(4,128)(2,1)S(1)}, bf16[4,64,128,64]{2,3,1,0:T(8,128)(2,1)}, /*index=5*/s32[]{:T(128)}, s32[]{:T(128)}, s32[]{:T(128)}) while((s32[]{:T(128)}, f32[64,128,64]{2,1,0:T(8,128)}, s32[]{:T(128)}, bf16[4,64]{1,0:T(4,128)(2,1)S(1)}, ...), condition=%wide.region_4.5_spmd, body=%wide.region_3.4_spmd.sunk | while | flops 1572933 | bytes 9437951 | solution.py:28
  128.4 4.6 %convert_add_fusion.3 = f32[64,128,64]{2,1,0:T(8,128)} fusion(f32[64,128,64]{2,1,0:T(8,128)} %get-tuple-element.215, bf16[1,64,128,64]{3,2,1,0:T(8,128)(2,1)S(1)} %copy.85, f32[64]{0:T(128)S(1)} %exponential_bitcast_fusion.3), kind=kLoop, calls=%fused_computation.clone.1 | loop fusion | flops 1572864 | bytes 5243136 | tf_op jit(solution)/shard_map/while/body/add | solution.py:38
  135.4 4.6 %convert_add_fusion.3 = f32[64,128,64]{2,1,0:T(8,128)} fusion(f32[64,128,64]{2,1,0:T(8,128)} %get-tuple-element.215, bf16[1,64,128,64]{3,2,1,0:T(8,128)(2,1)S(1)} %copy.85, f32[64]{0:T(128)S(1)} %exponential_bitcast_fusion.3), kind=kLoop, calls=%fused_computation.clone.1 | loop fusion | flops 1572864 | bytes 5243136 | tf_op jit(solution)/shard_map/while/body/add | solution.py:38
  142.4 4.6 %convert_add_fusion.3 = f32[64,128,64]{2,1,0:T(8,128)} fusion(f32[64,128,64]{2,1,0:T(8,128)} %get-tuple-element.215, bf16[1,64,128,64]{3,2,1,0:T(8,128)(2,1)S(1)} %copy.85, f32[64]{0:T(128)S(1)} %exponential_bitcast_fusion.3), kind=kLoop, calls=%fused_computation.clone.1 | loop fusion | flops 1572864 | bytes 5243136 | tf_op jit(solution)/shard_map/while/body/add | solution.py:38
  147.0 2.8 copy.57
  149.9 21.5 %while.25 = (s32[]{:T(128)}, f32[64,128,64]{1,2,0:T(8,128)S(1)}, f32[3,128,64,64]{1,3,2,0:T(8,128)}, f32[3,64]{1,0:T(4,128)}, f32[3,64,128,64]{2,3,1,0:T(8,128)}, /*index=5*/bf16[3,128,64,128]{3,1,2,0:T(8,128)(2,1)}, s32[]{:T(128)}) while((s32[]{:T(128)}, f32[64,128,64]{1,2,0:T(8,128)S(1)}, f32[3,128,64,64]{1,3,2,0:T(8,128)}, ...), condition=%wide.region_6.7_spmd, body=%wide.region_5.6_spmd.sunk | while | flops 135790592 | bytes 12584789 | solution.py:54
  149.9 4.5 %bitcast_dynamic-update-slice_fusion.2 = f32[3,128,64,64]{1,3,2,0:T(8,128)} fusion(f32[3,128,64,64]{1,3,2,0:T(8,128)} %get-tuple-element.239, s32[]{:T(128)} %get-tuple-element.237, bf16[3,128,64,128]{3,1,2,0:T(8,128)(2,1)} %get-tuple-element.249, f32[64,128,64]{1,2,0:T(8,128)S(1)} %get-tuple-element.238), kind=kOutput, calls=%fused_computation.3.clone.1 | convolution fusion | flops 134742016 | bytes 6292480 | tf_op jit(solution)/shard_map/while/body/eval_jaxpr/thn,hnp->thp/dot_general | solution.py:45
  155.1 2.0 bitcast_add_fusion.3
  157.1 4.5 %bitcast_dynamic-update-slice_fusion.2 = f32[3,128,64,64]{1,3,2,0:T(8,128)} fusion(f32[3,128,64,64]{1,3,2,0:T(8,128)} %get-tuple-element.239, s32[]{:T(128)} %get-tuple-element.237, bf16[3,128,64,128]{3,1,2,0:T(8,128)(2,1)} %get-tuple-element.249, f32[64,128,64]{1,2,0:T(8,128)S(1)} %get-tuple-element.238), kind=kOutput, calls=%fused_computation.3.clone.1 | convolution fusion | flops 134742016 | bytes 6292480 | tf_op jit(solution)/shard_map/while/body/eval_jaxpr/thn,hnp->thp/dot_general | solution.py:45
  162.2 2.0 bitcast_add_fusion.3
  164.2 4.5 %bitcast_dynamic-update-slice_fusion.2 = f32[3,128,64,64]{1,3,2,0:T(8,128)} fusion(f32[3,128,64,64]{1,3,2,0:T(8,128)} %get-tuple-element.239, s32[]{:T(128)} %get-tuple-element.237, bf16[3,128,64,128]{3,1,2,0:T(8,128)(2,1)} %get-tuple-element.249, f32[64,128,64]{1,2,0:T(8,128)S(1)} %get-tuple-element.238), kind=kOutput, calls=%fused_computation.3.clone.1 | convolution fusion | flops 134742016 | bytes 6292480 | tf_op jit(solution)/shard_map/while/body/eval_jaxpr/thn,hnp->thp/dot_general | solution.py:45
  169.4 2.0 bitcast_add_fusion.3
  173.3 12.8 %multiply_reduce_fusion.1 = (f32[3,128,64]{1,2,0:T(8,128)S(1)}, f32[3,128,64,64]{1,3,2,0:T(8,128)}) fusion(f32[3,128,64,64]{1,0,3,2:T(4,128)} %reshape.143, bf16[3,128,64,64]{1,3,2,0:T(8,128)(2,1)S(1)} %copy-done.1, f32[64]{0:T(128)S(1)} %bitcast.92, f32[3,128,64,64]{1,3,2,0:T(8,128)} %get-tuple-element.82, f32[3,64,128,128]{3,2,1,0:T(8,128)S(1)} %bitcast.79, ...), kind=kOutput, calls=%fused_computation.24 | convolution fusion | flops 438804480 | bytes 34914560 | tf_op jit(solution)/shard_map/khts,kshp->kthp/dot_general | solution.py:96
  186.1 11.9 %copy.59 = f32[3,128,64,64]{1,0,3,2:T(4,128)} copy(f32[3,128,64,64]{1,3,2,0:T(8,128)} %get-tuple-element.136) | data formatting | bytes 12582912 | tf_op jit(solution)/shard_map/add | solution.py:115
  198.0 10.9 %reshape.139 = f32[384,4,1024]{0,2,1:T(8,128)} reshape(f32[3,128,64,64]{1,0,3,2:T(4,128)} %copy.59) | data formatting | bytes 12582912 | tf_op jit(solution)/shard_map/reshape | solution.py:116
  209.1 5.7 %multiply_convert_fusion.5 = bf16[384,4,1024]{0,2,1:T(8,128)(2,1)S(1)} fusion(f32[384,4,1024]{0,2,1:T(8,128)} %reshape.139, f32[384,4,1024]{0,2,1:T(8,128)} %bitcast.76, f32[4,1024]{1,0:T(4,128)S(1)} %mul.161, f32[384,4]{0,1:T(4,128)S(1)} %add_rsqrt_fusion), kind=kLoop, calls=%fused_computation.23 | loop fusion | flops 12582912 | bytes 15751168 | tf_op jit(solution)/shard_map/convert_element_type | solution.py:121
  214.9 21.2 %fusion.20 = bf16[384,4096]{1,0:T(8,128)(2,1)} fusion(bf16[384,4096]{0,1:T(8,128)(2,1)S(1)} %bitcast.81, bf16[1,4096,4096]{2,1,0:T(8,128)(2,1)} %param.24), kind=kOutput, calls=%fused_computation.31 | convolution fusion | flops 12886474752 | bytes 39845888 | tf_op jit(solution)/shard_map/dot_general | solution.py:123
  236.1 44.5 %reduce-scatter.2.cloned.1.call-done = bf16[384,2048]{1,0:T(8,128)(2,1)} async-done(((bf16[384,4096]{1,0:T(8,128)(2,1)}), bf16[384,2048]{1,0:T(8,128)(2,1)}) %reduce-scatter.2.cloned.1.call-update) | async-done | bytes 1572880 | tf_op jit(solution)/shard_map/reduce_scatter | solution.py:124
  280.5 2.0 fusion.23
  282.6 19.8 %collective-permute-done = bf16[384,2048]{1,0:T(8,128)(2,1)S(1)} collective-permute-done((bf16[384,2048]{1,0:T(8,128)(2,1)S(1)}, bf16[384,2048]{1,0:T(8,128)(2,1)S(1)}, u32[]{:S(2)}, u32[]{:S(2)}) %collective-permute-start) | collective-permute-done | bytes 1572896 | tf_op jit(solution)/shard_map/ppermute | solution.py:34
  (81 shorter events, 30.9 us)
Async XLA Ops:
  6.5 9.9 %copy-start.3 = (bf16[1,384,4096]{2,1,0:T(8,128)(2,1)S(1)}, bf16[1,384,4096]{2,1,0:T(8,128)(2,1)}, u32[]{:S(2)}) copy-start(bf16[1,384,4096]{2,1,0:T(8,128)(2,1)} %param.15) | copy-start | bytes 9437188
  6.5 117.0 %all-gather.4.cloned.1.call-start = ((), (), s32[]{:S(2)}) async-start(), calls=%async_computation.2 | async-start | bytes 5242880 | tf_op jit(solution)/shard_map/all_gather | solution.py:14
  11.0 3.5 %copy-start.4 = (f32[3,128,64]{2,1,0:T(8,128)}, f32[3,128,64]{2,1,0:T(8,128)S(1)}, u32[]{:S(2)}) copy-start(f32[3,128,64]{2,1,0:T(8,128)S(1)} %reduce_window_sum.22) | copy-start | bytes 294916
  11.0 3.4 %copy-start.9 = (f32[3,64,1]{1,0,2:T(4,128)}, f32[3,64,1]{1,0,2:T(4,128)S(1)}, u32[]{:S(2)}) copy-start(f32[3,64,1]{1,0,2:T(4,128)S(1)} %copy.83) | copy-start | bytes 2308
  32.3 3.4 %copy-start = (bf16[3,128,64,64]{1,3,2,0:T(8,128)(2,1)}, bf16[3,128,64,64]{1,3,2,0:T(8,128)(2,1)S(1)}, u32[]{:S(2)}) copy-start(bf16[3,128,64,64]{1,3,2,0:T(8,128)(2,1)S(1)} %copy.50) | copy-start | bytes 9437188
  32.3 3.4 %copy-start.6 = (f32[3,128,64]{1,2,0:T(8,128)S(1)}, f32[3,128,64]{1,2,0:T(8,128)}, u32[]{:S(2)}) copy-start(f32[3,128,64]{1,2,0:T(8,128)} %copy.51) | copy-start | bytes 294916
  35.7 10.2 %copy-start.14 = (u32[32]{0:T(128)S(1)}, u32[32]{0:T(128)}, u32[]{:S(2)}) copy-start(u32[32]{0:T(128)} %constant.73) | copy-start | bytes 388
  44.2 236.4 %reduce-scatter.2.cloned.1.call-start = ((), (), s32[]{:S(2)}) async-start(), calls=%async_computation.1 | async-start | bytes 4718592 | tf_op jit(solution)/shard_map/reduce_scatter | solution.py:124
  65.5 11.0 %copy-start.10 = (f32[1,4096]{1,0:T(1,128)S(1)}, f32[1,4096]{1,0:T(1,128)}, u32[]{:S(2)}) copy-start(f32[1,4096]{1,0:T(1,128)} %param.23) | copy-start | bytes 49156
  80.7 45.3 %copy-start.13 = (bf16[4,64]{1,0:T(4,128)(2,1)S(1)}, bf16[4,64]{1,0:T(4,128)(2,1)}, u32[]{:S(2)}) copy-start(bf16[4,64]{1,0:T(4,128)(2,1)} %reshape.144) | copy-start | bytes 1540
  149.9 21.5 %copy-start.2 = (f32[3,4,128,128]{3,2,1,0:T(8,128)S(1)}, f32[3,4,128,128]{3,2,1,0:T(8,128)}, u32[]{:S(2)}) copy-start(f32[3,4,128,128]{3,2,1,0:T(8,128)} %fusion.24) | copy-start | bytes 2359300
  171.4 1.9 copy-start.1
  171.4 1.9 copy-start.7
  171.4 1.9 copy-start.8
  171.5 1.9 copy-start.11
  171.5 1.9 copy-start.12
  214.9 65.7 %copy-start.5 = (bf16[1,384,2048]{2,1,0:T(8,128)(2,1)S(1)}, bf16[1,384,2048]{2,1,0:T(8,128)(2,1)}, u32[]{:S(2)}) copy-start(bf16[1,384,2048]{2,1,0:T(8,128)(2,1)} %param.25) | copy-start | bytes 4718596
  282.5 19.9 %collective-permute-start = (bf16[384,2048]{1,0:T(8,128)(2,1)S(1)}, bf16[384,2048]{1,0:T(8,128)(2,1)S(1)}, u32[]{:S(2)}, u32[]{:S(2)}) collective-permute-start(bf16[384,2048]{1,0:T(8,128)(2,1)S(1)} %fusion.23), channel_id=1, source_target_pairs={{24,0},{0,8},{8,16},{16,24},{25,1},{1,9},{9,17},{17,25},{26,2},{2,... | collective-permute-start | bytes 4718600 | tf_op jit(solution)/shard_map/ppermute | solution.py:34
Sparse Core Ops, SparseCore 0:
  44.3 79.1 all-gather.3
  236.2 44.3 reduce-scatter.1
where the time goes:
time: 314 us; the launch traced here: 310 us
  waiting for transfers between devices  102 us (32%)
  local copies, waits for them, and re-layouts  89.5 us (29%)
  matrix products  57.1 us (18%)
  other arithmetic  39.4 us (13%)
  between operations  14.3 us (5%)
  blocking collectives  8.13 us (3%)
    reduce_scatter x1, waiting for transfers between devices, on_device(): lax.psum_scatter(partial_value.astype(jnp.bfloat16), 'tp', scatter_dimens...  44.5 us
    all_gather x1, waiting for transfers between devices, carried_in(): lax.all_gather(a.astype(kind), axis)  37.3 us
    dot_general x1, matrix products, on_device(): partial_value = jnp.dot(normed, weight, preferred_element_type=jnp.float32)  21.2 us
    ppermute x1, waiting for transfers between devices, passed_along(): return lax.ppermute(block, axis, route)  19.8 us
    another operation x2, local copies, waits for them, and re-layouts, on_device(): values_low = head_input[0].reshape(blocks, BLOCK, heads_local, HEAD_DIM)  15.8 us
    convert_element_type x2, local copies, waits for them, and re-layouts, on_device(): gated = scan_out * jax.nn.silu(gate_input[0].astype(jnp.float32))  15.8 us
    add x3, other arithmetic, link_states(): jnp.exp(latter[0])[:, None, None] * earlier[1] + latter[1]  13.8 us
    dot_general x3, matrix products, block_step(): jnp.einsum('thn,hnp->thp', map_blk, carried.astype(jnp.bfloat16), preferr...  13.5 us
  transfers between devices with their start and end apart: 3, of which 3 were waited for; matrix products, arithmetic and copies ran while one was open for 11% of the time, Pallas kernels for 0%

commit v1 on v0

v1 whole, which is shorter than its diff:
```python
import functools

import jax
import jax.numpy as jnp
from jax import lax
from jax.experimental import pallas as pl
from jax.experimental.pallas import tpu as pltpu
from jax.sharding import PartitionSpec as P

HEAD_DIM = 64
STATE = 128
BLOCK = 128
CHUNKS = 2
TILE = 256
MESH = pl.DeviceIdType.MESH
F32 = jnp.float32
BF16 = jnp.bfloat16


def parts_of(v, n):
    out = []
    for _ in range(n):
        hi = v.astype(BF16)
        out.append(hi)
        v = v - hi.astype(F32)
    return out


def dot(a, b):
    return jnp.dot(a, b, preferred_element_type=F32)


def lane_spread(v, onehot, n):
    return sum(dot(p, onehot) for p in parts_of(v, n))


def kernel(
    sizes,
    x_hbm,
    gate_hbm,
    b_ref,
    c_ref,
    raw_ref,
    bias_ref,
    rate_ref,
    skip_ref,
    gain_ref,
    w_hbm,
    res_hbm,
    o_ref,
    xv,
    gv,
    wv,
    rv,
    fx,
    fresh,
    total,
    st,
    onehot,
    rows,
    rowx,
    e_ref,
    f_ref,
    pin,
    pout,
    gbuf,
    nbuf,
    acc,
    sbuf,
    rbuf,
    fbuf,
    x_sem,
    g_sem,
    w_sem,
    r_sem,
    ps_sem,
    pr_sem,
    ts_sem,
    tr_sem,
    ss_sem,
    sr_sem,
):
    n_sec, n_ctx, n_tp = sizes
    length, width = x_hbm.shape
    model = w_hbm.shape[1]
    heads = raw_ref.shape[1]
    groups = b_ref.shape[1] // STATE
    gw = width // groups
    per_group = heads // groups
    blocks = length // BLOCK
    cw = gw // CHUNKS
    share = model // n_tp
    tiles = share // TILE
    sec = lax.axis_index("section")
    ctx = lax.axis_index("ctx")
    tp = lax.axis_index("tp")
    sec_next = lax.rem(sec + 1, n_sec)
    sec_prev = lax.rem(sec + n_sec - 1, n_sec)
    ctx_next = lax.rem(ctx + 1, n_ctx)
    ctx_prev = lax.rem(ctx + n_ctx - 1, n_ctx)
    first = ctx == 0
    has_next = ctx < n_ctx - 1

    def gcols(g):
        return pl.ds(pl.multiple_of(g * gw, gw), gw)

    def ccols(g, j):
        return pl.ds(pl.multiple_of(g * gw + j * cw, cw), cw)

    def krows(k):
        return pl.ds(k * BLOCK, BLOCK)

    def x_copy(g):
        return pltpu.make_async_copy(x_hbm.at[:, gcols(g)], xv.at[:, gcols(g)], x_sem.at[g])

    def w_copy(g):
        slot = lax.rem(g, 2)
        return pltpu.make_async_copy(
            w_hbm.at[pl.ds(pl.multiple_of(g * gw, gw), gw), :], wv.at[slot], w_sem.at[slot]
        )

    g_copy = pltpu.make_async_copy(gate_hbm, gv, g_sem)
    r_copy = pltpu.make_async_copy(res_hbm, rv, r_sem)

    barrier = pltpu.get_barrier_semaphore()
    greet = [{"ctx": ctx_next}, {"ctx": ctx_prev}, {"section": sec_next}, {"section": sec_prev}]
    greet += [{"tp": lax.rem(tp + o, n_tp)} for o in range(1, n_tp)]
    for who in greet:
        pl.semaphore_signal(barrier, inc=1, device_id=who, device_id_type=MESH)
    for g in range(groups):
        x_copy(g).start()
    g_copy.start()
    for g in range(min(2, groups)):
        w_copy(g).start()
    r_copy.start()

    at_row = lax.broadcasted_iota(jnp.int32, (BLOCK, BLOCK), 0)
    at_col = lax.broadcasted_iota(jnp.int32, (BLOCK, BLOCK), 1)
    lower = at_row >= at_col
    lower_one = jnp.where(lower, 1.0, 0.0).astype(BF16)
    rows[...] = jnp.zeros_like(rows)
    for k in range(blocks):
        v = raw_ref[krows(k), :] + bias_ref[...]
        step = jnp.maximum(v, 0.0) + jnp.log1p(jnp.exp(-jnp.abs(v)))
        decay = -rate_ref[...] * step
        cum = sum(dot(lower_one, p) for p in parts_of(decay, 3))
        mid = 0.5 * cum[BLOCK - 1 :, :]
        e_ref[krows(k), :] = jnp.exp(cum - mid)
        f_ref[krows(k), :] = step * jnp.exp(mid - cum)
        rows[k : k + 1, :] = jnp.exp(mid)
    rows[blocks : blocks + 1, :] = skip_ref[...]

    pl.semaphore_wait(barrier, len(greet))

    def p_copy(g, j):
        q = g * CHUNKS + j
        return pltpu.make_async_remote_copy(
            src_ref=pout.at[q],
            dst_ref=pin.at[q],
            send_sem=ps_sem.at[q],
            recv_sem=pr_sem.at[q],
            device_id={"ctx": ctx_next},
            device_id_type=MESH,
        )

    @pl.loop(0, groups)
    def _(g):
        head = lax.broadcasted_iota(jnp.int32, (heads, gw), 0)
        lane = lax.broadcasted_iota(jnp.int32, (heads, gw), 1)
        start = (head - g * per_group) * HEAD_DIM
        one = jnp.where((lane >= start) & (lane < start + HEAD_DIM), 1.0, 0.0).astype(BF16)
        onehot[:, gcols(g)] = one
        rowx[:, gcols(g)] = lane_spread(rows[...], one, 3)
        x_copy(g).wait()
        for j in range(CHUNKS):
            cols = ccols(g, j)
            for k in range(blocks):
                scale = lane_spread(f_ref[krows(k), :], onehot[:, cols], 2)
                scaled = (scale * xv[krows(k), cols].astype(F32)).astype(BF16)
                fx[krows(k), cols] = scaled
                b_blk = b_ref[krows(k), pl.ds(pl.multiple_of(g * STATE, STATE), STATE)]
                new = lax.dot_general(
                    b_blk, scaled, (((0,), (0,)), ((), ())), preferred_element_type=F32
                )
                q = rowx[k : k + 1, cols]
                new = new * q
                fresh[k, :, cols] = new
                if k == 0:
                    total[:, cols] = new
                else:
                    total[:, cols] = total[:, cols] * (q * q) + new

            @pl.when(first)
            def _():
                pin[g * CHUNKS + j] = jnp.zeros((STATE, cw), BF16)
                pout[g * CHUNKS + j] = total[:, cols].astype(BF16)
                p_copy(g, j).start()

    g_copy.wait()

    @pl.loop(0, length // BLOCK)
    def _(k):
        acc[pl.ds(pl.multiple_of(k * BLOCK, BLOCK), BLOCK), :] = jnp.zeros((BLOCK, model), F32)

    @pl.loop(0, groups)
    def _(g):
        for j in range(CHUNKS):
            cols = ccols(g, j)
            q = g * CHUNKS + j

            @pl.when(jnp.logical_not(first))
            def _():
                p_copy(g, j).wait_recv()

                @pl.when(has_next)
                def _():
                    whole = rowx[0:1, cols]
                    for k in range(1, blocks):
                        whole = whole * rowx[k : k + 1, cols]
                    out = total[:, cols] + pin[q].astype(F32) * (whole * whole)
                    pout[q] = out.astype(BF16)
                    p_copy(g, j).start()

            st[:, j * cw : (j + 1) * cw] = pin[q].astype(F32)

        for k in range(blocks):
            state_cols = pl.ds(pl.multiple_of(g * STATE, STATE), STATE)
            b_blk = b_ref[krows(k), state_cols]
            c_blk = c_ref[krows(k), state_cols]
            cb = lax.dot_general(
                c_blk, b_blk, (((1,), (1,)), ((), ())), preferred_element_type=F32
            )
            left = jnp.concatenate([jnp.where(lower, cb, 0.0).astype(BF16), c_blk], axis=1)
            squares = jnp.zeros((BLOCK, 1), F32)
            for j in range(CHUNKS):
                cols = ccols(g, j)
                here = slice(j * cw, (j + 1) * cw)
                q = rowx[k : k + 1, cols]
                state = st[:, here]
                right = jnp.concatenate([fx[krows(k), cols], (state * q).astype(BF16)], axis=0)
                y = dot(left, right) * lane_spread(e_ref[krows(k), :], onehot[:, cols], 2)
                y = y + rowx[blocks : blocks + 1, cols] * xv[krows(k), cols].astype(F32)
                gate = gv[krows(k), cols].astype(F32)
                y = y * (gate / (1.0 + jnp.exp(-gate)))
                gbuf[:, here] = y
                squares = squares + jnp.sum(y * y, axis=1, keepdims=True)
                if k < blocks - 1:
                    st[:, here] = state * (q * q) + fresh[k, :, cols]
            norm = lax.rsqrt(squares * (1.0 / gw) + 1e-05)
            nbuf[krows(k), :] = (gbuf[...] * norm * gain_ref[:, gcols(g)]).astype(BF16)

        w_copy(g).wait()

        @pl.when(g < groups - 1)
        def _():
            slot = lax.rem(g, 2)

            @pl.loop(0, model // TILE)
            def _(t):
                at = pl.ds(pl.multiple_of(t * TILE, TILE), TILE)
                acc[:, at] += dot(nbuf[...], wv[slot, :, at])

            @pl.when(g + 2 < groups)
            def _():
                w_copy(g + 2).start()

    last = (groups - 1) % 2

    def finished(at):
        return (acc[:, at] + dot(nbuf[...], wv[last, :, at])).astype(BF16)

    def t_copy(o, t):
        return pltpu.make_async_remote_copy(
            src_ref=sbuf.at[o - 1, t],
            dst_ref=rbuf.at[o - 1, t],
            send_sem=ts_sem.at[o - 1, t],
            recv_sem=tr_sem.at[o - 1, t],
            device_id={"tp": lax.rem(tp + o, n_tp)},
            device_id_type=MESH,
        )

    def s_copy(t):
        return pltpu.make_async_remote_copy(
            src_ref=fbuf.at[t],
            dst_ref=o_ref.at[:, pl.ds(pl.multiple_of(t * TILE, TILE), TILE)],
            send_sem=ss_sem.at[t],
            recv_sem=sr_sem.at[t],
            device_id={"section": sec_next},
            device_id_type=MESH,
        )

    @pl.loop(0, tiles)
    def _(t):
        for o in range(1, n_tp):
            peer = lax.rem(tp + o, n_tp)
            at = pl.ds(pl.multiple_of(peer * share + t * TILE, TILE), TILE)
            sbuf[o - 1, t] = finished(at)
            t_copy(o, t).start()

    r_copy.wait()

    @pl.loop(0, tiles)
    def _(t):
        at = pl.ds(pl.multiple_of(tp * share + t * TILE, TILE), TILE)
        here = pl.ds(pl.multiple_of(t * TILE, TILE), TILE)
        acc[:, at] = finished(at).astype(F32) + rv[:, here].astype(F32)

    @pl.loop(0, tiles)
    def _(t):
        at = pl.ds(pl.multiple_of(tp * share + t * TILE, TILE), TILE)
        mixed = acc[:, at]
        for o in range(1, n_tp):
            t_copy(o, t).wait_recv()
            mixed = mixed + rbuf[o - 1, t].astype(F32)
        fbuf[t] = mixed.astype(BF16)
        s_copy(t).start()

    @pl.when(has_next)
    def _():
        @pl.loop(0, groups)
        def _(g):
            for j in range(CHUNKS):
                p_copy(g, j).wait_send()

    @pl.loop(0, tiles)
    def _(t):
        for o in range(1, n_tp):
            t_copy(o, t).wait_send()
        s_copy(t).wait()


def on_device(
    sizes,
    head_input,
    gate_input,
    b_input,
    c_input,
    step_raw,
    step_bias,
    decay_rate,
    skip_scale,
    norm_gain,
    out_weight,
    residual,
):
    n_sec, n_ctx, n_tp = sizes
    length, width = head_input.shape[1:]
    model = out_weight.shape[2]
    heads = step_raw.shape[2]
    groups = b_input.shape[2] // STATE
    gw = width // groups
    blocks = length // BLOCK
    share = model // n_tp
    tiles = share // TILE
    row_count = (blocks + 1 + 7) // 8 * 8
    chunks = groups * CHUNKS
    dma = pltpu.SemaphoreType.DMA
    vmem = pl.BlockSpec(memory_space=pltpu.VMEM)
    anywhere = pl.BlockSpec(memory_space=pl.ANY)
    out = pl.pallas_call(
        functools.partial(kernel, sizes),
        out_shape=jax.ShapeDtypeStruct((length, share), BF16),
        in_specs=[anywhere, anywhere] + [vmem] * 7 + [anywhere, anywhere],
        out_specs=anywhere,
        scratch_shapes=[
            pltpu.VMEM((length, width), BF16),
            pltpu.VMEM((length, width), BF16),
            pltpu.VMEM((2, gw, model), BF16),
            pltpu.VMEM((length, share), BF16),
            pltpu.VMEM((length, width), BF16),
            pltpu.VMEM((blocks, STATE, width), F32),
            pltpu.VMEM((STATE, width), F32),
            pltpu.VMEM((STATE, gw), F32),
            pltpu.VMEM((heads, width), BF16),
            pltpu.VMEM((row_count, heads), F32),
            pltpu.VMEM((row_count, width), F32),
            pltpu.VMEM((length, heads), F32),
            pltpu.VMEM((length, heads), F32),
            pltpu.VMEM((chunks, STATE, gw // CHUNKS), BF16),
            pltpu.VMEM((chunks, STATE, gw // CHUNKS), BF16),
            pltpu.VMEM((BLOCK, gw), F32),
            pltpu.VMEM((length, gw), BF16),
            pltpu.VMEM((length, model), F32),
            pltpu.VMEM((n_tp - 1, tiles, length, TILE), BF16),
            pltpu.VMEM((n_tp - 1, tiles, length, TILE), BF16),
            pltpu.VMEM((tiles, length, TILE), BF16),
            dma((groups,)),
            dma,
            dma((2,)),
            dma,
            dma((chunks,)),
            dma((chunks,)),
            dma((n_tp - 1, tiles)),
            dma((n_tp - 1, tiles)),
            dma((tiles,)),
            dma((tiles,)),
        ],
        compiler_params=pltpu.CompilerParams(
            collective_id=0, has_side_effects=True, vmem_limit_bytes=63 * 1024 * 1024
        ),
    )(
        head_input[0],
        gate_input[0],
        b_input[0],
        c_input[0],
        step_raw[0],
        step_bias,
        decay_rate,
        skip_scale,
        norm_gain,
        out_weight[0],
        residual[0],
    )
    return out[None]


def solution(mesh):
    sizes = tuple(mesh.shape[name] for name in ("section", "ctx", "tp"))
    whole = P("section", "ctx", "tp")
    heads = P("section", "tp")
    placed = (whole,) * 5 + (heads,) * 4 + (P("section", "tp", None), whole)
    return jax.shard_map(
        functools.partial(on_device, sizes),
        mesh=mesh,
        in_specs=placed,
        out_specs=whole,
        check_vma=False,
    )
```

time: 314 us -> 91.4 us (0.29); the launches traced: 310 us -> 91.3 us
  waiting for transfers between devices: 102 us -> 0 us
  Pallas kernels: 0 us -> 86.8 us
  local copies, waits for them, and re-layouts: 89.5 us -> 4.43 us
  matrix products: 57.1 us -> 0 us
  other arithmetic: 39.4 us -> 0 us
  between operations: 14.3 us -> 0.01 us
  blocking collectives: 8.13 us -> 0 us
    pallas_call x0 -> x1, Pallas kernels: none -> 86.8 us  [on_device(): pl.pallas_call(functools.partial(kernel, sizes), out_shape=jax.ShapeDtype...]
    dot_general x7 -> x0, matrix products: 57.1 us -> none  [the longest x1 21.2 us: on_device(): partial_value = jnp.dot(normed, weight, preferred_element_type=jnp.float32)]
    reduce_scatter x1 -> x0, waiting for transfers between devices: 44.5 us -> none  [on_device(): lax.psum_scatter(partial_value.astype(jnp.bfloat16), 'tp', scatter_dimens...]
    all_gather x1 -> x0, waiting for transfers between devices: 37.3 us -> none  [carried_in(): lax.all_gather(a.astype(kind), axis)]
    ppermute x1 -> x0, waiting for transfers between devices: 19.8 us -> none  [passed_along(): return lax.ppermute(block, axis, route)]
    add x6 -> x0, other arithmetic: 19.8 us -> none  [the longest x3 13.8 us: link_states(): jnp.exp(latter[0])[:, None, None] * earlier[1] + latter[1]]
    another operation x4 -> x0, local copies, waits for them, and re-layouts: 18 us -> none  [the longest x2 15.8 us: on_device(): values_low = head_input[0].reshape(blocks, BLOCK, heads_local, HEAD_DIM)]
    convert_element_type x4 -> x0, local copies, waits for them, and re-layouts: 16.8 us -> none  [the longest x2 15.8 us: on_device(): gated = scan_out * jax.nn.silu(gate_input[0].astype(jnp.float32))]
  transfers between devices with their start and end apart: 3 -> 0, of which waited for: 3 -> 0; matrix products, arithmetic and copies ran while one was open for 11% -> 0% of each run, Pallas kernels for 0% -> 0%
where the time goes in v1:
time: 91.4 us; the launch traced here: 91.3 us
  Pallas kernels  86.8 us (95%)
  local copies, waits for them, and re-layouts  4.43 us (5%)
    pallas_call x1, Pallas kernels, on_device(): pl.pallas_call(functools.partial(kernel, sizes), out_shape=jax.ShapeDtype...  86.8 us
    unnamed x2, local copies, waits for them, and re-layouts  4.43 us

profile of v1, /device:TPU:26, one launch (start us, length us, event | category | flops | bytes accessed | tf_op | source)
XLA Modules:
  0.0 91.3 jit_solution(2804183019620622235)
XLA Ops:
  0.0 1.7 %copy.12 = f32[1,384,64]{2,1,0:T(8,128)} copy(f32[1,384,64]{1,2,0:T(8,128)} %param.15) | data formatting | bytes 196608 | tf_op args[4]
  1.7 86.8 %shard_map.109 = bf16[384,2048]{1,0:T(8,128)(2,1)} custom-call(bf16[384,4096]{1,0:T(8,128)(2,1)} %bitcast.10, bf16[384,4096]{1,0:T(8,128)(2,1)} %bitcast.11, bf16[384,512]{1,0:T(8,128)(2,1)} %bitcast.14, bf16[384,512]{1,0:T(8,128)(2,1)} %bitcast.15, f32[384,64]{1,0:T(8,128)} %bitcast.13, f32[1,64]{1,0:T(1,128)} %bias_ref.1, f32[1,64]{1,0:T(1,128)} %rate_ref.1, ...), custom_call_target="tpu_custom_call" | custom-call | tf_op jit(solution)/shard_map/pallas_call | solution.py:360
  88.5 2.7 %copy.14 = bf16[1,384,2048]{2,1,0:T(8,128)(2,1)} copy(bf16[1,384,2048]{2,1,0:T(8,128)(2,1)} %bitcast.9) | data formatting | bytes 3145728

commit v2 on v1

--- a/solution.py
+++ b/solution.py
@@ -30,8 +30,8 @@
     return jnp.dot(a, b, preferred_element_type=F32)
 
 
-def lane_spread(v, onehot, n):
-    return sum(dot(p, onehot) for p in parts_of(v, n))
+def halves(v):
+    return jnp.concatenate(parts_of(v, 2), axis=1)
 
 
 def kernel(
@@ -55,7 +55,7 @@
     fx,
     fresh,
     total,
-    st,
+    left,
     onehot,
     rows,
     rowx,
@@ -64,8 +64,6 @@
     pin,
     pout,
     gbuf,
-    nbuf,
-    acc,
     sbuf,
     rbuf,
     fbuf,
@@ -83,7 +81,7 @@
     n_sec, n_ctx, n_tp = sizes
     length, width = x_hbm.shape
     model = w_hbm.shape[1]
-    heads = raw_ref.shape[1]
+    heads = raw_ref.shape[0]
     groups = b_ref.shape[1] // STATE
     gw = width // groups
     per_group = heads // groups
@@ -113,11 +111,9 @@
     def x_copy(g):
         return pltpu.make_async_copy(x_hbm.at[:, gcols(g)], xv.at[:, gcols(g)], x_sem.at[g])
 
-    def w_copy(g):
-        slot = lax.rem(g, 2)
-        return pltpu.make_async_copy(
-            w_hbm.at[pl.ds(pl.multiple_of(g * gw, gw), gw), :], wv.at[slot], w_sem.at[slot]
-        )
+    def w_copy(o):
+        at = pl.ds(pl.multiple_of(lax.rem(tp + o, n_tp) * share, share), share)
+        return pltpu.make_async_copy(w_hbm.at[:, at], wv.at[:, at], w_sem.at[o])
 
     g_copy = pltpu.make_async_copy(gate_hbm, gv, g_sem)
     r_copy = pltpu.make_async_copy(res_hbm, rv, r_sem)
@@ -130,8 +126,8 @@
     for g in range(groups):
         x_copy(g).start()
     g_copy.start()
-    for g in range(min(2, groups)):
-        w_copy(g).start()
+    for o in range(n_tp):
+        w_copy((o + 1) % n_tp).start()
     r_copy.start()
 
     at_row = lax.broadcasted_iota(jnp.int32, (BLOCK, BLOCK), 0)
@@ -140,13 +136,13 @@
     lower_one = jnp.where(lower, 1.0, 0.0).astype(BF16)
     rows[...] = jnp.zeros_like(rows)
     for k in range(blocks):
-        v = raw_ref[krows(k), :] + bias_ref[...]
+        v = raw_ref[:, krows(k)].T + bias_ref[...]
         step = jnp.maximum(v, 0.0) + jnp.log1p(jnp.exp(-jnp.abs(v)))
         decay = -rate_ref[...] * step
         cum = sum(dot(lower_one, p) for p in parts_of(decay, 3))
         mid = 0.5 * cum[BLOCK - 1 :, :]
-        e_ref[krows(k), :] = jnp.exp(cum - mid)
-        f_ref[krows(k), :] = step * jnp.exp(mid - cum)
+        e_ref[krows(k), :] = halves(jnp.exp(cum - mid))
+        f_ref[krows(k), :] = halves(step * jnp.exp(mid - cum))
         rows[k : k + 1, :] = jnp.exp(mid)
     rows[blocks : blocks + 1, :] = skip_ref[...]
 
@@ -169,22 +165,23 @@
         lane = lax.broadcasted_iota(jnp.int32, (heads, gw), 1)
         start = (head - g * per_group) * HEAD_DIM
         one = jnp.where((lane >= start) & (lane < start + HEAD_DIM), 1.0, 0.0).astype(BF16)
+        one = jnp.concatenate([one, one], axis=0)
         onehot[:, gcols(g)] = one
-        rowx[:, gcols(g)] = lane_spread(rows[...], one, 3)
+        rowx[:, gcols(g)] = dot(halves(rows[...]), one)
         x_copy(g).wait()
         for j in range(CHUNKS):
             cols = ccols(g, j)
+            scale = dot(f_ref[...], onehot[:, cols])
+            fx[:, cols] = (scale * xv[:, cols].astype(F32)).astype(BF16)
             for k in range(blocks):
-                scale = lane_spread(f_ref[krows(k), :], onehot[:, cols], 2)
-                scaled = (scale * xv[krows(k), cols].astype(F32)).astype(BF16)
-                fx[krows(k), cols] = scaled
                 b_blk = b_ref[krows(k), pl.ds(pl.multiple_of(g * STATE, STATE), STATE)]
                 new = lax.dot_general(
-                    b_blk, scaled, (((0,), (0,)), ((), ())), preferred_element_type=F32
+                    b_blk, fx[krows(k), cols], (((0,), (0,)), ((), ())), preferred_element_type=F32
                 )
                 q = rowx[k : k + 1, cols]
                 new = new * q
-                fresh[k, :, cols] = new
+                if k < blocks - 1:
+                    fresh[k, :, cols] = new
                 if k == 0:
                     total[:, cols] = new
                 else:
@@ -196,17 +193,29 @@
                 pout[g * CHUNKS + j] = total[:, cols].astype(BF16)
                 p_copy(g, j).start()
 
-    g_copy.wait()
-
-    @pl.loop(0, length // BLOCK)
-    def _(k):
-        acc[pl.ds(pl.multiple_of(k * BLOCK, BLOCK), BLOCK), :] = jnp.zeros((BLOCK, model), F32)
-
     @pl.loop(0, groups)
     def _(g):
+        state_cols = pl.ds(pl.multiple_of(g * STATE, STATE), STATE)
+        for k in range(blocks):
+            c_blk = c_ref[krows(k), state_cols]
+            cb = lax.dot_general(
+                c_blk,
+                b_ref[krows(k), state_cols],
+                (((1,), (1,)), ((), ())),
+                preferred_element_type=F32,
+            )
+            left[g, krows(k), :STATE] = jnp.where(lower, cb, 0.0).astype(BF16)
+            left[g, krows(k), STATE:] = c_blk
+
+    g_copy.wait()
+
+    @pl.loop(0, groups)
+    def _(g):
+        squares = [jnp.zeros((BLOCK, 1), F32) for _ in range(blocks)]
         for j in range(CHUNKS):
             cols = ccols(g, j)
-            q = g * CHUNKS + j
+            here = slice(j * cw, (j + 1) * cw)
+            chunk = g * CHUNKS + j
 
             @pl.when(jnp.logical_not(first))
             def _():
@@ -217,57 +226,29 @@
                     whole = rowx[0:1, cols]
                     for k in range(1, blocks):
                         whole = whole * rowx[k : k + 1, cols]
-                    out = total[:, cols] + pin[q].astype(F32) * (whole * whole)
-                    pout[q] = out.astype(BF16)
+                    out = total[:, cols] + pin[chunk].astype(F32) * (whole * whole)
+                    pout[chunk] = out.astype(BF16)
                     p_copy(g, j).start()
 
-            st[:, j * cw : (j + 1) * cw] = pin[q].astype(F32)
-
+            state = pin[chunk].astype(F32)
+            spread = dot(e_ref[...], onehot[:, cols])
+            for k in range(blocks):
+                q = rowx[k : k + 1, cols]
+                right = jnp.concatenate([fx[krows(k), cols], (state * q).astype(BF16)], axis=0)
+                y = dot(left[g, krows(k), :], right) * spread[k * BLOCK : (k + 1) * BLOCK]
+                y = y + rowx[blocks : blocks + 1, cols] * xv[krows(k), cols].astype(F32)
+                half = 0.5 * gv[krows(k), cols].astype(F32)
+                y = y * (half + half * jnp.tanh(half))
+                gbuf[krows(k), here] = y
+                squares[k] = squares[k] + jnp.sum(y * y, axis=1, keepdims=True)
+                if k < blocks - 1:
+                    state = state * (q * q) + fresh[k, :, cols]
         for k in range(blocks):
-            state_cols = pl.ds(pl.multiple_of(g * STATE, STATE), STATE)
-            b_blk = b_ref[krows(k), state_cols]
-            c_blk = c_ref[krows(k), state_cols]
-            cb = lax.dot_general(
-                c_blk, b_blk, (((1,), (1,)), ((), ())), preferred_element_type=F32
-            )
-            left = jnp.concatenate([jnp.where(lower, cb, 0.0).astype(BF16), c_blk], axis=1)
-            squares = jnp.zeros((BLOCK, 1), F32)
-            for j in range(CHUNKS):
-                cols = ccols(g, j)
-                here = slice(j * cw, (j + 1) * cw)
-                q = rowx[k : k + 1, cols]
-                state = st[:, here]
-                right = jnp.concatenate([fx[krows(k), cols], (state * q).astype(BF16)], axis=0)
-                y = dot(left, right) * lane_spread(e_ref[krows(k), :], onehot[:, cols], 2)
-                y = y + rowx[blocks : blocks + 1, cols] * xv[krows(k), cols].astype(F32)
-                gate = gv[krows(k), cols].astype(F32)
-                y = y * (gate / (1.0 + jnp.exp(-gate)))
-                gbuf[:, here] = y
-                squares = squares + jnp.sum(y * y, axis=1, keepdims=True)
-                if k < blocks - 1:
-                    st[:, here] = state * (q * q) + fresh[k, :, cols]
-            norm = lax.rsqrt(squares * (1.0 / gw) + 1e-05)
-            nbuf[krows(k), :] = (gbuf[...] * norm * gain_ref[:, gcols(g)]).astype(BF16)
-
-        w_copy(g).wait()
-
-        @pl.when(g < groups - 1)
-        def _():
-            slot = lax.rem(g, 2)
-
-            @pl.loop(0, model // TILE)
-            def _(t):
-                at = pl.ds(pl.multiple_of(t * TILE, TILE), TILE)
-                acc[:, at] += dot(nbuf[...], wv[slot, :, at])
-
-            @pl.when(g + 2 < groups)
-            def _():
-                w_copy(g + 2).start()
-
-    last = (groups - 1) % 2
+            norm = lax.rsqrt(squares[k] * (1.0 / gw) + 1e-05)
+            gv[krows(k), gcols(g)] = (gbuf[krows(k), :] * norm * gain_ref[:, gcols(g)]).astype(BF16)
 
     def finished(at):
-        return (acc[:, at] + dot(nbuf[...], wv[last, :, at])).astype(BF16)
+        return dot(gv[...], wv[:, at]).astype(BF16)
 
     def t_copy(o, t):
         return pltpu.make_async_remote_copy(
@@ -289,6 +270,9 @@
             device_id_type=MESH,
         )
 
+    for o in range(1, n_tp):
+        w_copy(o).wait()
+
     @pl.loop(0, tiles)
     def _(t):
         for o in range(1, n_tp):
@@ -297,20 +281,18 @@
             sbuf[o - 1, t] = finished(at)
             t_copy(o, t).start()
 
+    w_copy(0).wait()
     r_copy.wait()
 
     @pl.loop(0, tiles)
     def _(t):
         at = pl.ds(pl.multiple_of(tp * share + t * TILE, TILE), TILE)
         here = pl.ds(pl.multiple_of(t * TILE, TILE), TILE)
-        acc[:, at] = finished(at).astype(F32) + rv[:, here].astype(F32)
-
-    @pl.loop(0, tiles)
-    def _(t):
-        at = pl.ds(pl.multiple_of(tp * share + t * TILE, TILE), TILE)
-        mixed = acc[:, at]
+        fbuf[t] = finished(at)
         for o in range(1, n_tp):
             t_copy(o, t).wait_recv()
+        mixed = rv[:, here].astype(F32) + fbuf[t].astype(F32)
+        for o in range(1, n_tp):
             mixed = mixed + rbuf[o - 1, t].astype(F32)
         fbuf[t] = mixed.astype(BF16)
         s_copy(t).start()
@@ -365,28 +347,26 @@
         scratch_shapes=[
             pltpu.VMEM((length, width), BF16),
             pltpu.VMEM((length, width), BF16),
-            pltpu.VMEM((2, gw, model), BF16),
+            pltpu.VMEM((width, model), BF16),
             pltpu.VMEM((length, share), BF16),
             pltpu.VMEM((length, width), BF16),
-            pltpu.VMEM((blocks, STATE, width), F32),
+            pltpu.VMEM((max(blocks - 1, 1), STATE, width), F32),
             pltpu.VMEM((STATE, width), F32),
-            pltpu.VMEM((STATE, gw), F32),
-            pltpu.VMEM((heads, width), BF16),
+            pltpu.VMEM((groups, length, 2 * STATE), BF16),
+            pltpu.VMEM((2 * heads, width), BF16),
             pltpu.VMEM((row_count, heads), F32),
             pltpu.VMEM((row_count, width), F32),
-            pltpu.VMEM((length, heads), F32),
-            pltpu.VMEM((length, heads), F32),
+            pltpu.VMEM((length, 2 * heads), BF16),
+            pltpu.VMEM((length, 2 * heads), BF16),
             pltpu.VMEM((chunks, STATE, gw // CHUNKS), BF16),
             pltpu.VMEM((chunks, STATE, gw // CHUNKS), BF16),
-            pltpu.VMEM((BLOCK, gw), F32),
-            pltpu.VMEM((length, gw), BF16),
-            pltpu.VMEM((length, model), F32),
+            pltpu.VMEM((length, gw), F32),
             pltpu.VMEM((n_tp - 1, tiles, length, TILE), BF16),
             pltpu.VMEM((n_tp - 1, tiles, length, TILE), BF16),
             pltpu.VMEM((tiles, length, TILE), BF16),
             dma((groups,)),
             dma,
-            dma((2,)),
+            dma((n_tp,)),
             dma,
             dma((chunks,)),
             dma((chunks,)),
@@ -396,14 +376,14 @@
             dma((tiles,)),
         ],
         compiler_params=pltpu.CompilerParams(
-            collective_id=0, has_side_effects=True, vmem_limit_bytes=63 * 1024 * 1024
+            collective_id=0, has_side_effects=True, vmem_limit_bytes=67043328
         ),
     )(
         head_input[0],
         gate_input[0],
         b_input[0],
         c_input[0],
-        step_raw[0],
+        step_raw[0].T,
         step_bias,
         decay_rate,
         skip_scale,

time: 91.4 us -> 78.9 us (0.86)
  Pallas kernels: 86.8 us -> 75.3 us
  local copies, waits for them, and re-layouts: 4.43 us -> 2.73 us
    pallas_call x1, Pallas kernels: 86.8 us -> 75.3 us  [on_device(): pl.pallas_call(functools.partial(kernel, sizes), out_shape=jax.ShapeDtype...]
    unnamed x2 -> x1, local copies, waits for them, and re-layouts: 4.43 us -> 2.73 us
where the time goes in v2:
time: 78.9 us; the launch traced here: 78 us
  Pallas kernels  75.3 us (95%)
  local copies, waits for them, and re-layouts  2.73 us (3%)
    pallas_call x1, Pallas kernels, on_device(): pl.pallas_call(functools.partial(kernel, sizes), out_shape=jax.ShapeDtype...  75.3 us
    unnamed x1, local copies, waits for them, and re-layouts  2.73 us

profile of v2, /device:TPU:26, one launch (start us, length us, event | category | flops | bytes accessed | tf_op | source)
XLA Modules:
  0.0 78.0 jit_solution(15560076911085150300)
XLA Ops:
  0.0 75.3 %shard_map.109 = bf16[384,2048]{1,0:T(8,128)(2,1)} custom-call(bf16[384,4096]{1,0:T(8,128)(2,1)} %bitcast.12, bf16[384,4096]{1,0:T(8,128)(2,1)} %bitcast.13, bf16[384,512]{1,0:T(8,128)(2,1)} %bitcast.15, bf16[384,512]{1,0:T(8,128)(2,1)} %bitcast.16, f32[64,384]{1,0:T(8,128)} %bitcast.17, f32[1,64]{1,0:T(1,128)} %bias_ref.1, f32[1,64]{1,0:T(1,128)} %rate_ref.1, ...), custom_call_target="tpu_custom_call" | custom-call | tf_op jit(solution)/shard_map/pallas_call | solution.py:342
  75.3 2.7 %copy.13 = bf16[1,384,2048]{2,1,0:T(8,128)(2,1)} copy(bf16[1,384,2048]{2,1,0:T(8,128)(2,1)} %bitcast.11) | data formatting | bytes 3145728
